TPU v7x, 32 devices: a whole 2x2x4 slice. The times are simulated.
32 devices in a mesh: tm: 2 (over core), space: 16 (over z, y, x).
Axes of the slice: x: 2, y: 2, z: 4, core: 2. Of those that a mesh axis runs over, the one named last changes fastest.
Arguments:
- checkpoints: float32 [2, 5, 2048, 128], P('tm', None, 'space'), may hold values from -6 to 6
- sources: float32 [2, 5, 2048, 128], P(None, None, 'space'), may hold values from -3 to 3
- pitch: float32 [8], replicated, may hold values from -3.140625 to 3.140625
- metric: float32 [2048, 128], P('space'), may hold values from 0.5 to 2
- obj_weight: float32 [5, 2048, 128], P(None, 'space'), may hold values from 0.1 to 0.6
- adjoint_end: float32 [5, 2048, 128], P(None, 'space'), may hold values from -6 to 6
- lift: bfloat16 [5, 128, 128], replicated, may hold values from -0.5 to 0.5
- mixing: float32 [5, 5, 5], replicated, may hold values from -1.25 to 1.25
- faces: int32 [2048, 4], P('space'), may hold values from 0 to 191
- send_idx: int32 [16, 4, 16], P('space'), may hold values from 0 to 127
Outputs:
- adjoint_bounds: float32 [2, 5, 2048, 128], P('tm', None, 'space')
- pitch_grad: float32 [8], replicated
Inputs may be any that keep to these rules, and one draw needn't show every extreme that they name: `faces`: values below 128 name the subdomain's own blocks; value 128 + d * 16 + s names slot s of the blocks received from direction d. `send_idx`: entry [p, d, s] is a local block of subdomain p sent to subdomain p + o[d], o = (1, -1, 2, -2); blocks may repeat.
All inputs are finite; a program needn't handle non-finite values.
Results may differ from a plain program's by a relative error of at most 0.0035.
Values may be sent and summed in bfloat16 or wider, within the bound.
A program may use at most 64 MiB of HBM per device.

v0:
```python
import functools
import math

import jax
import jax.numpy as jnp
from jax import lax
from jax.experimental import pallas as pl
from jax.experimental.pallas import tpu as pltpu
from jax.sharding import PartitionSpec as P

OFFSETS = (1, -1, 2, -2)
STEP_SIZE = 0.5
F32 = jnp.float32
BF16 = jnp.bfloat16
MESH = pl.DeviceIdType.MESH


def dot(a, b):
    return jnp.dot(a, b, preferred_element_type=F32)


def window_kernel(
    dims,
    pitch_ref, mixing_ref, cp_hbm, src_hbm, metric_hbm, weight_hbm, end_hbm, lift_ref, faces_ref, send_ref,
    out_ref, grad_ref,
    u_ref, src_ref, metric_ref, weight_ref, a_ref, hand_ref, base_ref, dd_ref, wu_ref, lift_t, sq_ref,
    p_own, p_halo, pt_own, pt_halo, pick, pick_t, out_buf, in_buf, back_out, back_in, y_ref, yh_ref, z_ref,
    mixed_ref, g_ref, gw_ref, gh_ref, row_ref, rows_ref,
    load_sems, send_sems, recv_sems, bsend_sems, brecv_sems, hand_sems, gsend_sems, grecv_sems,
):
    comps, blocks, nodes, slots, halo, half, n_tm, n_space, norm = dims
    ghosts = 4 * halo
    faces_n = slots - 1
    wide = comps * nodes
    tm = lax.axis_index("tm")
    sp = lax.axis_index("space")
    n_dev = n_tm * n_space
    me = tm * n_space + sp

    loads = [
        pltpu.make_async_copy(cp_hbm.at[0], u_ref, load_sems.at[0]),
        pltpu.make_async_copy(src_hbm, src_ref, load_sems.at[1]),
        pltpu.make_async_copy(metric_hbm, metric_ref, load_sems.at[2]),
        pltpu.make_async_copy(weight_hbm, weight_ref, load_sems.at[3]),
        pltpu.make_async_copy(end_hbm, a_ref, load_sems.at[4]),
    ]
    for load in loads:
        load.start()

    in_buf[...] = jnp.zeros_like(in_buf)
    back_in[...] = jnp.zeros_like(back_in)

    barrier = pltpu.get_barrier_semaphore()

    def greet(r, carry):
        other = lax.rem(me + r, n_dev)
        pl.semaphore_signal(
            barrier, inc=1, device_id=(other // n_space, lax.rem(other, n_space)), device_id_type=MESH
        )
        return carry

    lax.fori_loop(1, n_dev, greet, 0)

    row_ids = lax.broadcasted_iota(jnp.int32, (blocks, blocks), 0)
    lane_ids = lax.broadcasted_iota(jnp.int32, (blocks, blocks), 1)
    face_cols = []
    for k in range(faces_n):
        col = jnp.broadcast_to(faces_ref[:, k : k + 1], (blocks, blocks))
        face_cols.append(col)
        p_own[k * blocks : (k + 1) * blocks, :] = (col == lane_ids).astype(F32).astype(BF16)
        turned = jnp.transpose(col.astype(F32)).astype(jnp.int32)
        pt_own[k * blocks : (k + 1) * blocks, :] = (turned == row_ids).astype(F32).astype(BF16)
        hit = (turned[:ghosts] == row_ids[:ghosts] + blocks).astype(F32).astype(BF16)
        pt_halo[k * ghosts : (k + 1) * ghosts, :blocks] = hit
        pt_halo[k * ghosts : (k + 1) * ghosts, blocks:] = hit
    for pair in range(faces_n // 2):
        low = lane_ids < ghosts
        col = jnp.where(low, face_cols[2 * pair], face_cols[2 * pair + 1])
        want = jnp.where(low, lane_ids, lane_ids - ghosts) + blocks
        p_halo[:, pair * 2 * ghosts : (pair + 1) * 2 * ghosts] = (col == want).astype(F32).astype(BF16)
    wanted = jnp.concatenate(
        [send_ref[0, d : d + 1, :] for d in range(4)] + [jnp.full((1, blocks - ghosts), -1, jnp.int32)], axis=1
    )
    spread = jnp.broadcast_to(wanted, (blocks, blocks))
    pick_t[...] = (spread == row_ids).astype(F32).astype(BF16)[:, :ghosts]
    spread_t = jnp.transpose(spread.astype(F32)).astype(jnp.int32)
    pick[...] = (spread_t[:ghosts] == lane_ids[:ghosts]).astype(F32).astype(BF16)
    for k in range(slots):
        lift_t[:, k * nodes : (k + 1) * nodes] = jnp.transpose(lift_ref[k].astype(F32)).astype(BF16)
    row_ref[...] = jnp.zeros_like(row_ref)

    loads[0].wait()

    def lanes(c):
        return slice(c * nodes, (c + 1) * nodes)

    def target(shift):
        return (tm, jnp.clip(sp + shift, 0, n_space - 1))

    def inside(shift):
        return (sp + shift >= 0) & (sp + shift < n_space)

    def forward_copy(n, d):
        rows = pl.ds(d * halo, halo)
        return pltpu.make_async_remote_copy(
            src_ref=out_buf.at[n, rows], dst_ref=in_buf.at[n, rows],
            send_sem=send_sems.at[n, d], recv_sem=recv_sems.at[n, d],
            device_id=target(OFFSETS[d]), device_id_type=MESH,
        )

    def backward_copy(n, d):
        rows = pl.ds(d * halo, halo)
        return pltpu.make_async_remote_copy(
            src_ref=back_out.at[n, rows], dst_ref=back_in.at[n, rows],
            send_sem=bsend_sems.at[n, d], recv_sem=brecv_sems.at[n, d],
            device_id=target(-OFFSETS[d]), device_id_type=MESH,
        )

    def coef(k, e, c):
        return mixing_ref[(k * comps + e) * comps + c]

    def turn_of(level):
        angle = jnp.full((8, nodes), pitch_ref[level], F32)
        return jnp.cos(angle)[0:1], jnp.sin(angle)[0:1]

    pl.semaphore_wait(barrier, n_dev - 1)

    chunk = 32

    def forward(n, carry):
        level = tm * half + n
        active = (n < half - 1) | (tm == n_tm - 1)

        @pl.when(active)
        def _():
            for c in range(comps):
                sq_ref[:, lanes(c)] = jnp.tanh(u_ref[c]).astype(BF16)
            out_buf[n] = dot(pick[...], sq_ref[...]).astype(BF16)
            for d in range(4):
                @pl.when(inside(OFFSETS[d]))
                def _():
                    forward_copy(n, d).start()

        @pl.when(n == 0)
        def _():
            for load in loads[1:]:
                load.wait()

        keep = jnp.where(level > 0, 1.0, 0.0).astype(F32)
        for c in range(comps):
            state = u_ref[c]
            t = jnp.tanh(state)
            dd_ref[n, c] = STEP_SIZE * (1.0 - t * t)
            wu_ref[n, c] = (keep * weight_ref[c]) * state

        @pl.when(active)
        def _():
            cosine, sine = turn_of(level)
            squashed = sq_ref[...]
            for k in range(slots):
                if k == 0:
                    got = squashed
                else:
                    got = dot(p_own[(k - 1) * blocks : k * blocks, :], squashed).astype(BF16)
                stacked = jnp.concatenate([got[:, lanes(c)] for c in range(comps)], axis=0)
                y_ref[k] = dot(stacked, lift_t[:, lanes(k)])

            def own_mix(r, carry):
                start = pl.multiple_of(r * chunk, chunk)
                metric_half = STEP_SIZE * metric_ref[pl.ds(start, chunk), :]
                sums = [None] * comps
                for k in range(slots):
                    for c in range(comps):
                        term = y_ref[k, pl.ds(c * blocks + start, chunk), :]
                        for e in range(comps):
                            add = coef(k, e, c) * term
                            sums[e] = add if sums[e] is None else sums[e] + add
                for e in range(comps):
                    rows = pl.ds(start, chunk)
                    forcing = cosine * src_ref[0, e, rows, :] + sine * src_ref[1, e, rows, :]
                    base_ref[e, rows, :] = u_ref[e, rows, :] + STEP_SIZE * forcing - metric_half * sums[e]
                return carry

            lax.fori_loop(0, blocks // chunk, own_mix, 0)

            for d in range(4):
                @pl.when(inside(-OFFSETS[d]))
                def _():
                    forward_copy(n, d).wait_recv()

            ghost = in_buf[n]
            stacked = jnp.concatenate([ghost[:, lanes(c)] for c in range(comps)], axis=0)
            yh_ref[...] = dot(stacked, lift_t[:, nodes:])
            for k in range(1, slots):
                for part in range(ghosts // chunk):
                    for e in range(comps):
                        total = None
                        for c in range(comps):
                            at = c * ghosts + part * chunk
                            add = coef(k, e, c) * yh_ref[at : at + chunk, lanes(k - 1)]
                            total = add if total is None else total + add
                        at = (k - 1) * ghosts + part * chunk
                        z_ref[at : at + chunk, lanes(e)] = total.astype(BF16)
            more = dot(p_halo[...], z_ref[...])
            half_metric = STEP_SIZE * metric_ref[...]
            for e in range(comps):
                u_ref[e] = base_ref[e] - half_metric * more[:, lanes(e)]
            for d in range(4):
                @pl.when(inside(OFFSETS[d]))
                def _():
                    forward_copy(n, d).wait_send()

        return carry

    lax.fori_loop(0, half, forward, 0)

    def hand_copy():
        return pltpu.make_async_remote_copy(
            src_ref=a_ref, dst_ref=hand_ref, send_sem=hand_sems.at[0], recv_sem=hand_sems.at[1],
            device_id=(lax.rem(tm + n_tm - 1, n_tm), sp), device_id_type=MESH,
        )

    @pl.when(tm == n_tm - 1)
    def _():
        for c in range(comps):
            a_ref[c] = a_ref[c] + weight_ref[c] * u_ref[c]

    @pl.when(tm < n_tm - 1)
    def _():
        hand_copy().wait_recv()
        for c in range(comps):
            a_ref[c] = hand_ref[c]

    def grad_copy(r):
        other = lax.rem(me + r, n_dev)
        return pltpu.make_async_remote_copy(
            src_ref=row_ref, dst_ref=rows_ref.at[me], send_sem=gsend_sems.at[other], recv_sem=grecv_sems.at[me],
            device_id=(other // n_space, lax.rem(other, n_space)), device_id_type=MESH,
        )

    def backward(j, carry):
        n = half - 1 - j
        level = tm * half + n

        for e in range(comps):
            w = metric_ref[...] * a_ref[e]
            high = w.astype(BF16)
            sq_ref[:, lanes(e)] = high
            mixed_ref[0, :, lanes(e)] = (w - high.astype(F32)).astype(BF16)
        gw_ref[...] = dot(pt_halo[...], jnp.concatenate([sq_ref[...], mixed_ref[0]], axis=0))
        for k in range(1, slots):
            for part in range(ghosts // chunk):
                at = (k - 1) * ghosts + part * chunk
                for c in range(comps):
                    total = None
                    for e in range(comps):
                        add = coef(k, e, c) * gw_ref[at : at + chunk, lanes(e)]
                        total = add if total is None else total + add
                    to = c * ghosts + part * chunk
                    gh_ref[to : to + chunk, lanes(k - 1)] = total.astype(BF16)
        lifted = dot(gh_ref[...], lift_ref[1:].reshape(faces_n * nodes, nodes)).astype(BF16)
        for c in range(comps):
            back_out[n, :, lanes(c)] = lifted[c * ghosts : (c + 1) * ghosts]
        for d in range(4):
            @pl.when(inside(-OFFSETS[d]))
            def _():
                backward_copy(n, d).start()

        cosine, sine = turn_of(level)
        sums = None
        for e in range(comps):
            part = a_ref[e] * (cosine * src_ref[1, e] - sine * src_ref[0, e])
            sums = part if sums is None else sums + part
        value = jnp.sum(jnp.sum(sums, axis=0, keepdims=True), axis=1, keepdims=True) * (STEP_SIZE / norm)
        spots = lax.broadcasted_iota(jnp.int32, (1, nodes), 1)
        row_ref[...] = row_ref[...] + jnp.where(spots == level, value, 0.0)

        @pl.when(n == 0)
        def _():
            def tell(r, carry):
                grad_copy(r).start()
                return carry

            lax.fori_loop(1, n_dev, tell, 0)

        def own_mix(r, carry):
            start = pl.multiple_of(r * chunk, chunk)
            rows = pl.ds(start, chunk)
            weighted = [metric_ref[rows, :] * a_ref[e, rows, :] for e in range(comps)]
            for k in range(slots):
                for c in range(comps):
                    total = None
                    for e in range(comps):
                        add = coef(k, e, c) * weighted[e]
                        total = add if total is None else total + add
                    mixed_ref[k, rows, lanes(c)] = total.astype(BF16)
            return carry

        lax.fori_loop(0, blocks // chunk, own_mix, 0)
        for k in range(slots):
            if k == 0:
                got = mixed_ref[0]
            else:
                got = dot(pt_own[(k - 1) * blocks : k * blocks, :], mixed_ref[k]).astype(BF16)
            for c in range(comps):
                g_ref[c * blocks : (c + 1) * blocks, lanes(k)] = got[:, lanes(c)]
        pushed = dot(g_ref[...], lift_ref[...].reshape(slots * nodes, nodes))
        for c in range(comps):
            base_ref[c] = a_ref[c] + wu_ref[n, c] - dd_ref[n, c] * pushed[c * blocks : (c + 1) * blocks]

        for d in range(4):
            @pl.when(inside(OFFSETS[d]))
            def _():
                backward_copy(n, d).wait_recv()

        more = dot(pick_t[...], back_in[n])
        for c in range(comps):
            a_ref[c] = base_ref[c] - dd_ref[n, c] * more[:, lanes(c)]
        for d in range(4):
            @pl.when(inside(-OFFSETS[d]))
            def _():
                backward_copy(n, d).wait_send()
        return carry

    lax.fori_loop(0, half, backward, 0)

    @pl.when(tm > 0)
    def _():
        hand_copy().start()

    for c in range(comps):
        out_ref[0, c] = a_ref[c]

    def settle(r, carry):
        other = lax.rem(me + r, n_dev)
        pltpu.make_async_remote_copy(
            src_ref=row_ref, dst_ref=rows_ref.at[other], send_sem=gsend_sems.at[other],
            recv_sem=grecv_sems.at[other], device_id=(other // n_space, lax.rem(other, n_space)),
            device_id_type=MESH,
        ).wait()
        return carry

    lax.fori_loop(1, n_dev, settle, 0)
    rows_ref[me] = row_ref[...]
    grad_ref[...] = jnp.sum(rows_ref[...], axis=0)[:, : grad_ref.shape[1]]

    @pl.when(tm > 0)
    def _():
        hand_copy().wait_send()


def shards(
    checkpoints, sources, pitch, metric, obj_weight, adjoint_end, lift, mixing, faces, send_idx
):
    comps = sources.shape[1]
    blocks, nodes = metric.shape
    slots = lift.shape[0]
    halo = send_idx.shape[2]
    n_tm = lax.axis_size("tm")
    n_space = lax.axis_size("space")
    levels = pitch.shape[0]
    half = levels // n_tm
    ghosts = 4 * halo
    norm = math.sqrt(comps * nodes * blocks * n_space)
    wide = comps * nodes
    field = (comps, blocks, nodes)
    vmem = pl.BlockSpec(memory_space=pltpu.VMEM)
    smem = pl.BlockSpec(memory_space=pltpu.SMEM)
    anym = pl.BlockSpec(memory_space=pl.ANY)
    dma = pltpu.SemaphoreType.DMA
    n_dev = n_tm * n_space
    dims = (comps, blocks, nodes, slots, halo, half, n_tm, n_space, norm)
    bounds, grad = pl.pallas_call(
        functools.partial(window_kernel, dims),
        out_shape=(
            jax.ShapeDtypeStruct((1, *field), F32),
            jax.ShapeDtypeStruct((1, levels), F32),
        ),
        in_specs=[smem, smem, anym, anym, anym, anym, anym, vmem, vmem, vmem],
        out_specs=(vmem, vmem),
        scratch_shapes=[
            pltpu.VMEM(field, F32),
            pltpu.VMEM((2, *field), F32),
            pltpu.VMEM((blocks, nodes), F32),
            pltpu.VMEM(field, F32),
            pltpu.VMEM(field, F32),
            pltpu.VMEM(field, F32),
            pltpu.VMEM(field, F32),
            pltpu.VMEM((half, *field), F32),
            pltpu.VMEM((half, *field), F32),
            pltpu.VMEM((nodes, slots * nodes), BF16),
            pltpu.VMEM((blocks, wide), BF16),
            pltpu.VMEM(((slots - 1) * blocks, blocks), BF16),
            pltpu.VMEM((blocks, (slots - 1) * ghosts), BF16),
            pltpu.VMEM(((slots - 1) * blocks, blocks), BF16),
            pltpu.VMEM(((slots - 1) * ghosts, 2 * blocks), BF16),
            pltpu.VMEM((ghosts, blocks), BF16),
            pltpu.VMEM((blocks, ghosts), BF16),
            pltpu.VMEM((half, ghosts, wide), BF16),
            pltpu.VMEM((half, ghosts, wide), BF16),
            pltpu.VMEM((half, ghosts, wide), BF16),
            pltpu.VMEM((half, ghosts, wide), BF16),
            pltpu.VMEM((slots, comps * blocks, nodes), F32),
            pltpu.VMEM((comps * ghosts, (slots - 1) * nodes), F32),
            pltpu.VMEM(((slots - 1) * ghosts, wide), BF16),
            pltpu.VMEM((slots, blocks, wide), BF16),
            pltpu.VMEM((comps * blocks, slots * nodes), BF16),
            pltpu.VMEM(((slots - 1) * ghosts, wide), F32),
            pltpu.VMEM((comps * ghosts, (slots - 1) * nodes), BF16),
            pltpu.VMEM((1, nodes), F32),
            pltpu.VMEM((n_dev, 1, nodes), F32),
            dma((5,)),
            dma((half, 4)),
            dma((half, 4)),
            dma((half, 4)),
            dma((half, 4)),
            dma((2,)),
            dma((n_dev,)),
            dma((n_dev,)),
        ],
        compiler_params=pltpu.CompilerParams(
            collective_id=0, has_side_effects=True, vmem_limit_bytes=48 * 1024 * 1024
        ),
        name="window",
    )(pitch, mixing.reshape(-1), checkpoints, sources, metric, obj_weight, adjoint_end, lift, faces, send_idx)
    return bounds, grad.reshape(-1)


def solution(mesh):
    placed = (
        P("tm", None, "space", None),
        P(None, None, "space", None),
        P(),
        P("space", None),
        P(None, "space", None),
        P(None, "space", None),
        P(),
        P(),
        P("space", None),
        P("space", None, None),
    )
    return jax.shard_map(
        shards,
        mesh=mesh,
        in_specs=placed,
        out_specs=(P("tm", None, "space", None), P()),
        check_vma=False,
    )
```

profile of v0, /device:TPU:0, one launch (start us, length us, event | category | flops | bytes accessed | tf_op | source)
XLA Modules:
  0.0 67.0 jit_solution(17210728191807497657)
XLA Ops:
  0.6 0.0 copy-start.8
  0.6 0.0 copy-start.5
  0.7 0.9 %reshape.10.mixing_ref = f32[125]{0:T(128)S(1)} reshape(f32[5,5,5]{2,1,0:T(8,128)} %param.17) | data formatting | bytes 1000 | tf_op jit(solution)/shard_map/reshape | solution.py:425
  1.5 0.0 copy-done.8
  1.5 0.0 copy-start.6
  1.5 0.0 copy-start.7
  1.5 0.1 copy.12.faces_ref
  1.7 0.0 copy-done.5
  1.7 0.5 copy-done.6
  2.2 0.0 copy-done.7
  2.2 0.0 copy-start
  2.2 1.1 %copy-done = f32[2,5,128,128]{3,2,1,0:T(8,128)S(1)} copy-done((f32[2,5,128,128]{3,2,1,0:T(8,128)S(1)}, f32[2,5,128,128]{3,2,1,0:T(8,128)}, u32[]{:S(2)}) %copy-start) | copy-done | bytes 655384
  3.3 0.0 copy-start.1
  3.3 1.0 %copy-done.1 = f32[1,5,128,128]{3,2,1,0:T(8,128)S(1)} copy-done((f32[1,5,128,128]{3,2,1,0:T(8,128)S(1)}, f32[1,5,128,128]{3,2,1,0:T(8,128)}, u32[]{:S(2)}) %copy-start.1) | copy-done | bytes 327704
  4.3 0.0 copy-start.2
  4.3 1.0 %copy-done.2 = f32[5,128,128]{2,1,0:T(8,128)S(1)} copy-done((f32[5,128,128]{2,1,0:T(8,128)S(1)}, f32[5,128,128]{2,1,0:T(8,128)}, u32[]{:S(2)}) %copy-start.2) | copy-done | bytes 327704
  5.2 0.0 copy-start.3
  5.2 1.0 %copy-done.3 = f32[5,128,128]{2,1,0:T(8,128)S(1)} copy-done((f32[5,128,128]{2,1,0:T(8,128)S(1)}, f32[5,128,128]{2,1,0:T(8,128)}, u32[]{:S(2)}) %copy-start.3) | copy-done | bytes 327704
  6.2 0.0 copy-start.4
  6.2 0.9 %copy-done.4 = bf16[5,128,128]{2,1,0:T(8,128)(2,1)S(1)} copy-done((bf16[5,128,128]{2,1,0:T(8,128)(2,1)S(1)}, bf16[5,128,128]{2,1,0:T(8,128)(2,1)}, u32[]{:S(2)}) %copy-start.4) | copy-done | bytes 163864
  7.1 58.6 %window.1 = (f32[1,5,128,128]{3,2,1,0:T(8,128)S(1)}, f32[1,8]{1,0:T(1,128)S(1)}) custom-call(f32[8]{0:T(128)S(1)} %copy-done.7, f32[125]{0:T(128)S(1)} %reshape.10.mixing_ref, f32[1,5,128,128]{3,2,1,0:T(8,128)S(1)} %copy-done.1, f32[2,5,128,128]{3,2,1,0:T(8,128)S(1)} %copy-done, f32[128,128]{1,0:T(8,128)S(1)} %copy-done.5, f32[5,128,128]{2,1,0:T(8,128)S(1)} %copy-done.2, ...), custom_call_target="tpu_custom_call" | custom-call | tf_op jit(solution)/shard_map/window/pallas_call | solution.py:373
  65.7 0.7 %copy.15 = f32[1,5,128,128]{3,2,1,0:T(8,128)} copy(f32[1,5,128,128]{3,2,1,0:T(8,128)S(1)} %get-tuple-element.8) | data formatting | bytes 655360
  66.5 0.5 copy.16
Async XLA Ops:
  0.6 0.9 %copy-start.8 = (s32[128,4]{0,1:T(4,128)S(1)}, s32[128,4]{0,1:T(4,128)}, u32[]{:S(2)}) copy-start(s32[128,4]{0,1:T(4,128)} %param.18) | copy-start | bytes 6148
  0.6 1.0 %copy-start.5 = (f32[128,128]{1,0:T(8,128)S(1)}, f32[128,128]{1,0:T(8,128)}, u32[]{:S(2)}) copy-start(f32[128,128]{1,0:T(8,128)} %metric_hbm.1) | copy-start | bytes 196612
  1.5 0.7 %copy-start.6 = (s32[1,4,16]{2,1,0:T(4,128)S(1)}, s32[1,4,16]{2,1,0:T(4,128)}, u32[]{:S(2)}) copy-start(s32[1,4,16]{2,1,0:T(4,128)} %send_ref.1) | copy-start | bytes 772
  1.5 0.7 %copy-start.7 = (f32[8]{0:T(128)S(1)}, f32[8]{0:T(128)}, u32[]{:S(2)}) copy-start(f32[8]{0:T(128)} %pitch_ref.1) | copy-start | bytes 100
  2.2 1.1 %copy-start = (f32[2,5,128,128]{3,2,1,0:T(8,128)S(1)}, f32[2,5,128,128]{3,2,1,0:T(8,128)}, u32[]{:S(2)}) copy-start(f32[2,5,128,128]{3,2,1,0:T(8,128)} %src_hbm.1) | copy-start | bytes 1966084
  3.3 1.0 %copy-start.1 = (f32[1,5,128,128]{3,2,1,0:T(8,128)S(1)}, f32[1,5,128,128]{3,2,1,0:T(8,128)}, u32[]{:S(2)}) copy-start(f32[1,5,128,128]{3,2,1,0:T(8,128)} %cp_hbm.1) | copy-start | bytes 983044
  4.3 1.0 %copy-start.2 = (f32[5,128,128]{2,1,0:T(8,128)S(1)}, f32[5,128,128]{2,1,0:T(8,128)}, u32[]{:S(2)}) copy-start(f32[5,128,128]{2,1,0:T(8,128)} %weight_hbm.1) | copy-start | bytes 983044
  5.2 1.0 %copy-start.3 = (f32[5,128,128]{2,1,0:T(8,128)S(1)}, f32[5,128,128]{2,1,0:T(8,128)}, u32[]{:S(2)}) copy-start(f32[5,128,128]{2,1,0:T(8,128)} %end_hbm.1) | copy-start | bytes 983044
  6.2 0.9 %copy-start.4 = (bf16[5,128,128]{2,1,0:T(8,128)(2,1)S(1)}, bf16[5,128,128]{2,1,0:T(8,128)(2,1)}, u32[]{:S(2)}) copy-start(bf16[5,128,128]{2,1,0:T(8,128)(2,1)} %lift_ref.1) | copy-start | bytes 491524
where the time goes:
time: 67.3 us; the launch traced here: 67 us
  Pallas kernels  58.6 us (87%)
  local copies, waits for them, and re-layouts  7.68 us (11%)
  between operations  0.69 us (1%)
    pallas_call x1, Pallas kernels, shards(): pl.pallas_call(functools.partial(window_kernel, dims), out_shape=(jax.Sha...  58.6 us
    unnamed x21, local copies, waits for them, and re-layouts  6.83 us

commit v1 on v0

--- a/solution.py
+++ b/solution.py
@@ -21,12 +21,12 @@
 
 def window_kernel(
     dims,
-    pitch_ref, mixing_ref, cp_hbm, src_hbm, metric_hbm, weight_hbm, end_hbm, lift_ref, faces_ref, send_ref,
+    pitch_ref, mixing_ref, cp_hbm, src_hbm, metric_hbm, weight_hbm, end_hbm, lift_hbm, faces_hbm, send_hbm,
     out_ref, grad_ref,
-    u_ref, src_ref, metric_ref, weight_ref, a_ref, hand_ref, base_ref, dd_ref, wu_ref, lift_t, sq_ref,
+    u_ref, lift_ref, faces_ref, send_ref, src_ref, metric_ref, weight_ref, a_ref, hand_ref, base_ref, dd_ref, wu_ref, lift_t, sq_ref,
     p_own, p_halo, pt_own, pt_halo, pick, pick_t, out_buf, in_buf, back_out, back_in, y_ref, yh_ref, z_ref,
     mixed_ref, g_ref, gw_ref, gh_ref, row_ref, rows_ref,
-    load_sems, send_sems, recv_sems, bsend_sems, brecv_sems, hand_sems, gsend_sems, grecv_sems,
+    load_sems, send_sems, recv_sems, bsend_sems, brecv_sems, hand_sems, factor_sems, gsend_sems, grecv_sems,
 ):
     comps, blocks, nodes, slots, halo, half, n_tm, n_space, norm = dims
     ghosts = 4 * halo
@@ -36,9 +36,16 @@
     sp = lax.axis_index("space")
     n_dev = n_tm * n_space
     me = tm * n_space + sp
+    lead = tm == n_tm - 1
+    partner = (n_tm - 1 - tm, sp)
+    segment = tm
+    levels = half * n_tm
 
     loads = [
+        pltpu.make_async_copy(send_hbm, send_ref, load_sems.at[5]),
+        pltpu.make_async_copy(faces_hbm, faces_ref, load_sems.at[6]),
         pltpu.make_async_copy(cp_hbm.at[0], u_ref, load_sems.at[0]),
+        pltpu.make_async_copy(lift_hbm, lift_ref, load_sems.at[7]),
         pltpu.make_async_copy(src_hbm, src_ref, load_sems.at[1]),
         pltpu.make_async_copy(metric_hbm, metric_ref, load_sems.at[2]),
         pltpu.make_async_copy(weight_hbm, weight_ref, load_sems.at[3]),
@@ -61,14 +68,16 @@
 
     lax.fori_loop(1, n_dev, greet, 0)
 
+    for load in loads[:2]:
+        load.wait()
     row_ids = lax.broadcasted_iota(jnp.int32, (blocks, blocks), 0)
     lane_ids = lax.broadcasted_iota(jnp.int32, (blocks, blocks), 1)
     face_cols = []
     for k in range(faces_n):
-        col = jnp.broadcast_to(faces_ref[:, k : k + 1], (blocks, blocks))
+        turned = jnp.broadcast_to(faces_ref[k : k + 1, :], (blocks, blocks))
+        col = jnp.transpose(turned.astype(F32)).astype(jnp.int32)
         face_cols.append(col)
         p_own[k * blocks : (k + 1) * blocks, :] = (col == lane_ids).astype(F32).astype(BF16)
-        turned = jnp.transpose(col.astype(F32)).astype(jnp.int32)
         pt_own[k * blocks : (k + 1) * blocks, :] = (turned == row_ids).astype(F32).astype(BF16)
         hit = (turned[:ghosts] == row_ids[:ghosts] + blocks).astype(F32).astype(BF16)
         pt_halo[k * ghosts : (k + 1) * ghosts, :blocks] = hit
@@ -85,11 +94,8 @@
     pick_t[...] = (spread == row_ids).astype(F32).astype(BF16)[:, :ghosts]
     spread_t = jnp.transpose(spread.astype(F32)).astype(jnp.int32)
     pick[...] = (spread_t[:ghosts] == lane_ids[:ghosts]).astype(F32).astype(BF16)
-    for k in range(slots):
-        lift_t[:, k * nodes : (k + 1) * nodes] = jnp.transpose(lift_ref[k].astype(F32)).astype(BF16)
     row_ref[...] = jnp.zeros_like(row_ref)
-
-    loads[0].wait()
+    loads[2].wait()
 
     def lanes(c):
         return slice(c * nodes, (c + 1) * nodes)
@@ -117,21 +123,39 @@
         )
 
     def coef(k, e, c):
-        return mixing_ref[(k * comps + e) * comps + c]
+        return mixing_ref[k, e, c]
 
     def turn_of(level):
         angle = jnp.full((8, nodes), pitch_ref[level], F32)
         return jnp.cos(angle)[0:1], jnp.sin(angle)[0:1]
 
+    for c in range(comps):
+        sq_ref[:, lanes(c)] = jnp.tanh(u_ref[c]).astype(BF16)
+    out_buf[0] = dot(pick[...], sq_ref[...]).astype(BF16)
     pl.semaphore_wait(barrier, n_dev - 1)
+    for d in range(4):
+        @pl.when(inside(OFFSETS[d]))
+        def _():
+            forward_copy(0, d).start()
 
     chunk = 32
+    for load in loads[3:]:
+        load.wait()
+    for k in range(slots):
+        lift_t[:, k * nodes : (k + 1) * nodes] = jnp.transpose(lift_ref[k].astype(F32)).astype(BF16)
+
+    def factor_copy(level, which):
+        ref = (dd_ref, wu_ref)[which]
+        return pltpu.make_async_remote_copy(
+            src_ref=ref.at[level], dst_ref=ref.at[level], send_sem=factor_sems.at[0, which, level],
+            recv_sem=factor_sems.at[1, which, level], device_id=partner, device_id_type=MESH,
+        )
 
     def forward(n, carry):
-        level = tm * half + n
-        active = (n < half - 1) | (tm == n_tm - 1)
-
-        @pl.when(active)
+        level = segment * half + n
+        active = (n < half - 1) | lead
+
+        @pl.when(active & (n > 0))
         def _():
             for c in range(comps):
                 sq_ref[:, lanes(c)] = jnp.tanh(u_ref[c]).astype(BF16)
@@ -141,17 +165,17 @@
                 def _():
                     forward_copy(n, d).start()
 
-        @pl.when(n == 0)
-        def _():
-            for load in loads[1:]:
-                load.wait()
-
         keep = jnp.where(level > 0, 1.0, 0.0).astype(F32)
         for c in range(comps):
             state = u_ref[c]
             t = jnp.tanh(state)
-            dd_ref[n, c] = STEP_SIZE * (1.0 - t * t)
-            wu_ref[n, c] = (keep * weight_ref[c]) * state
+            dd_ref[level, c] = STEP_SIZE * (1.0 - t * t)
+            wu_ref[level, c] = (keep * weight_ref[c]) * state
+
+        @pl.when(jnp.logical_not(lead))
+        def _():
+            factor_copy(level, 0).start()
+            factor_copy(level, 1).start()
 
         @pl.when(active)
         def _():
@@ -216,31 +240,23 @@
 
     def hand_copy():
         return pltpu.make_async_remote_copy(
-            src_ref=a_ref, dst_ref=hand_ref, send_sem=hand_sems.at[0], recv_sem=hand_sems.at[1],
-            device_id=(lax.rem(tm + n_tm - 1, n_tm), sp), device_id_type=MESH,
-        )
-
-    @pl.when(tm == n_tm - 1)
-    def _():
-        for c in range(comps):
-            a_ref[c] = a_ref[c] + weight_ref[c] * u_ref[c]
-
-    @pl.when(tm < n_tm - 1)
-    def _():
-        hand_copy().wait_recv()
-        for c in range(comps):
-            a_ref[c] = hand_ref[c]
-
-    def grad_copy(r):
-        other = lax.rem(me + r, n_dev)
+            src_ref=a_ref, dst_ref=out_ref.at[0], send_sem=hand_sems.at[0], recv_sem=hand_sems.at[1],
+            device_id=partner, device_id_type=MESH,
+        )
+
+    def keep_copy():
+        return pltpu.make_async_copy(hand_ref, out_ref.at[0], hand_sems.at[2])
+
+    def grad_copy(source, other):
         return pltpu.make_async_remote_copy(
-            src_ref=row_ref, dst_ref=rows_ref.at[me], send_sem=gsend_sems.at[other], recv_sem=grecv_sems.at[me],
-            device_id=(other // n_space, lax.rem(other, n_space)), device_id_type=MESH,
+            src_ref=row_ref, dst_ref=rows_ref.at[source], send_sem=gsend_sems.at[other],
+            recv_sem=grecv_sems.at[source], device_id=(other // n_space, lax.rem(other, n_space)),
+            device_id_type=MESH,
         )
 
     def backward(j, carry):
-        n = half - 1 - j
-        level = tm * half + n
+        level = levels - 1 - j
+        n = level
 
         for e in range(comps):
             w = metric_ref[...] * a_ref[e]
@@ -266,6 +282,11 @@
             def _():
                 backward_copy(n, d).start()
 
+        @pl.when(level < half)
+        def _():
+            factor_copy(level, 0).wait_recv()
+            factor_copy(level, 1).wait_recv()
+
         cosine, sine = turn_of(level)
         sums = None
         for e in range(comps):
@@ -278,7 +299,7 @@
         @pl.when(n == 0)
         def _():
             def tell(r, carry):
-                grad_copy(r).start()
+                grad_copy(sp, lax.rem(me + r, n_dev)).start()
                 return carry
 
             lax.fori_loop(1, n_dev, tell, 0)
@@ -320,33 +341,57 @@
             @pl.when(inside(-OFFSETS[d]))
             def _():
                 backward_copy(n, d).wait_send()
+
+        @pl.when(level == half)
+        def _():
+            for c in range(comps):
+                hand_ref[c] = a_ref[c]
+            keep_copy().start()
+
         return carry
 
-    lax.fori_loop(0, half, backward, 0)
-
-    @pl.when(tm > 0)
+    @pl.when(lead)
     def _():
+        for c in range(comps):
+            a_ref[c] = a_ref[c] + weight_ref[c] * u_ref[c]
+        lax.fori_loop(0, levels, backward, 0)
         hand_copy().start()
-
-    for c in range(comps):
-        out_ref[0, c] = a_ref[c]
-
-    def settle(r, carry):
-        other = lax.rem(me + r, n_dev)
-        pltpu.make_async_remote_copy(
-            src_ref=row_ref, dst_ref=rows_ref.at[other], send_sem=gsend_sems.at[other],
-            recv_sem=grecv_sems.at[other], device_id=(other // n_space, lax.rem(other, n_space)),
-            device_id_type=MESH,
-        ).wait()
-        return carry
-
-    lax.fori_loop(1, n_dev, settle, 0)
-    rows_ref[me] = row_ref[...]
-    grad_ref[...] = jnp.sum(rows_ref[...], axis=0)[:, : grad_ref.shape[1]]
-
-    @pl.when(tm > 0)
+        rows_ref[sp] = row_ref[...]
+
+        def settle(r, carry):
+            other = lax.rem(sp + r, n_space)
+            grad_copy(other, me).wait_recv()
+            return carry
+
+        lax.fori_loop(1, n_space, settle, 0)
+
+    @pl.when(jnp.logical_not(lead))
+    def _():
+        def settle(r, carry):
+            grad_copy(r, me).wait_recv()
+            return carry
+
+        lax.fori_loop(0, n_space, settle, 0)
+
+    grad_ref[...] = jnp.sum(rows_ref[...], axis=0)[0, : grad_ref.shape[0]]
+
+    @pl.when(lead)
     def _():
         hand_copy().wait_send()
+        keep_copy().wait()
+
+        def sent(r, carry):
+            grad_copy(sp, lax.rem(me + r, n_dev)).wait_send()
+            return carry
+
+        lax.fori_loop(1, n_dev, sent, 0)
+
+    @pl.when(jnp.logical_not(lead))
+    def _():
+        hand_copy().wait_recv()
+        for level in range(half):
+            factor_copy(level, 0).wait_send()
+            factor_copy(level, 1).wait_send()
 
 
 def shards(
@@ -374,20 +419,23 @@
         functools.partial(window_kernel, dims),
         out_shape=(
             jax.ShapeDtypeStruct((1, *field), F32),
-            jax.ShapeDtypeStruct((1, levels), F32),
+            jax.ShapeDtypeStruct((levels,), F32),
         ),
-        in_specs=[smem, smem, anym, anym, anym, anym, anym, vmem, vmem, vmem],
-        out_specs=(vmem, vmem),
+        in_specs=[smem, smem] + [anym] * 8,
+        out_specs=(anym, vmem),
         scratch_shapes=[
             pltpu.VMEM(field, F32),
+            pltpu.VMEM(lift.shape, BF16),
+            pltpu.VMEM(faces.shape[::-1], jnp.int32),
+            pltpu.VMEM(send_idx.shape, jnp.int32),
             pltpu.VMEM((2, *field), F32),
             pltpu.VMEM((blocks, nodes), F32),
             pltpu.VMEM(field, F32),
             pltpu.VMEM(field, F32),
             pltpu.VMEM(field, F32),
             pltpu.VMEM(field, F32),
-            pltpu.VMEM((half, *field), F32),
-            pltpu.VMEM((half, *field), F32),
+            pltpu.VMEM((levels, *field), F32),
+            pltpu.VMEM((levels, *field), F32),
             pltpu.VMEM((nodes, slots * nodes), BF16),
             pltpu.VMEM((blocks, wide), BF16),
             pltpu.VMEM(((slots - 1) * blocks, blocks), BF16),
@@ -398,8 +446,8 @@
             pltpu.VMEM((blocks, ghosts), BF16),
             pltpu.VMEM((half, ghosts, wide), BF16),
             pltpu.VMEM((half, ghosts, wide), BF16),
-            pltpu.VMEM((half, ghosts, wide), BF16),
-            pltpu.VMEM((half, ghosts, wide), BF16),
+            pltpu.VMEM((levels, ghosts, wide), BF16),
+            pltpu.VMEM((levels, ghosts, wide), BF16),
             pltpu.VMEM((slots, comps * blocks, nodes), F32),
             pltpu.VMEM((comps * ghosts, (slots - 1) * nodes), F32),
             pltpu.VMEM(((slots - 1) * ghosts, wide), BF16),
@@ -408,22 +456,23 @@
             pltpu.VMEM(((slots - 1) * ghosts, wide), F32),
             pltpu.VMEM((comps * ghosts, (slots - 1) * nodes), BF16),
             pltpu.VMEM((1, nodes), F32),
-            pltpu.VMEM((n_dev, 1, nodes), F32),
-            dma((5,)),
+            pltpu.VMEM((n_space, 1, nodes), F32),
+            dma((8,)),
             dma((half, 4)),
             dma((half, 4)),
-            dma((half, 4)),
-            dma((half, 4)),
-            dma((2,)),
+            dma((levels, 4)),
+            dma((levels, 4)),
+            dma((3,)),
+            dma((2, 2, half)),
             dma((n_dev,)),
-            dma((n_dev,)),
+            dma((n_space,)),
         ],
         compiler_params=pltpu.CompilerParams(
-            collective_id=0, has_side_effects=True, vmem_limit_bytes=48 * 1024 * 1024
+            collective_id=0, has_side_effects=True, vmem_limit_bytes=60 * 1024 * 1024
         ),
         name="window",
-    )(pitch, mixing.reshape(-1), checkpoints, sources, metric, obj_weight, adjoint_end, lift, faces, send_idx)
-    return bounds, grad.reshape(-1)
+    )(pitch, mixing, checkpoints, sources, metric, obj_weight, adjoint_end, lift, faces.T, send_idx)
+    return bounds, grad
 
 
 def solution(mesh):

time: 67.3 us -> 57.5 us (0.85)
  local copies, waits for them, and re-layouts: 7.68 us -> 2.23 us
  Pallas kernels: 58.6 us -> 54.3 us
    unnamed x21 -> x4, local copies, waits for them, and re-layouts: 6.83 us -> 2.23 us
    pallas_call x1, Pallas kernels: 58.6 us -> 54.3 us  [shards(): pl.pallas_call(functools.partial(window_kernel, dims), out_shape=(jax.Sha...]
    reshape x1 -> x0, local copies, waits for them, and re-layouts: 0.85 us -> none  [shards(): mixing.reshape(-1)]
where the time goes in v1:
time: 57.5 us; the launch traced here: 57.2 us
  Pallas kernels  54.3 us (94%)
  local copies, waits for them, and re-layouts  2.23 us (4%)
  between operations  0.65 us (1%)
    pallas_call x1, Pallas kernels, shards(): pl.pallas_call(functools.partial(window_kernel, dims), out_shape=(jax.Sha...  54.3 us
    unnamed x4, local copies, waits for them, and re-layouts  2.23 us

profile of v1, /device:TPU:0, one launch (start us, length us, event | category | flops | bytes accessed | tf_op | source)
XLA Modules:
  0.0 57.2 jit_solution(21571065214977280)
XLA Ops:
  0.6 54.3 %window.1 = (f32[1,5,128,128]{3,2,1,0:T(8,128)}, f32[8]{0:T(128)}) custom-call(f32[8]{0:T(128)} %pitch_ref.1, f32[5,5,5]{2,1,0:T(8,128)} %mixing_ref.1, f32[1,5,128,128]{3,2,1,0:T(8,128)} %cp_hbm.1, f32[2,5,128,128]{3,2,1,0:T(8,128)} %src_hbm.1, f32[128,128]{1,0:T(8,128)} %metric_hbm.1, f32[5,128,128]{2,1,0:T(8,128)} %weight_hbm.1, f32[5,128,128]{2,1,0:T(8,128)} %end_hbm.1, ...), custom_call_target="tpu_custom_call" | custom-call | tf_op jit(solution)/shard_map/window/pallas_call | solution.py:418
  55.0 0.0 copy-start
  55.0 1.7 %copy.14 = f32[1,5,128,128]{3,2,1,0:T(8,128)} copy(f32[1,5,128,128]{3,2,1,0:T(8,128)} %get-tuple-element.4) | data formatting | bytes 655360
  56.7 0.0 copy-done
  56.7 0.5 copy.15
Async XLA Ops:
  55.0 1.7 %copy-start = (f32[8]{0:T(128)S(1)}, f32[8]{0:T(128)}, u32[]{:S(2)}) copy-start(f32[8]{0:T(128)} %get-tuple-element.5) | copy-start | bytes 100
